TPU v7x, 32 devices: a whole 2x2x4 slice. The times are simulated.
32 devices in a mesh: samp: 16 (over z, y, core), snp: 2 (over x).
Axes of the slice: x: 2, y: 2, z: 4, core: 2. Of those that a mesh axis runs over, the one named last changes fastest.
Arguments:
- genotype: int32 [16384, 4096], P('samp', 'snp'), may hold values from 0 to 3, as said below
- basis: bfloat16 [4096, 40], P('snp'), may hold values from -6 to 6
Outputs:
- sample_scores: bfloat16 [16384, 40], P('samp')
- snp_block: float32 [4096, 40], P('snp')
Inputs may be any that keep to these rules, and one draw needn't show every extreme that they name: `genotype`: the value 3 marks a missing call; 0, 1 and 2 are dosages.
All inputs are finite; a program needn't handle non-finite values.
Results may differ from a plain program's by a relative error of at most 0.0065.
Values may be sent and summed in bfloat16 or wider, within the bound.
A program may use at most 64 MiB of HBM per device.

v0:
```python
import jax
import jax.numpy as jnp
from jax import lax
from jax.sharding import PartitionSpec as P

ITERS = 2


def per_device(genotype, basis):
    observed = genotype < 3
    dosage = jnp.where(observed, genotype, 0).astype(jnp.float32)
    allele_sum, called = lax.psum(
        (jnp.sum(dosage, axis=0), jnp.sum(observed.astype(jnp.float32), axis=0)), "samp"
    )
    freq = (allele_sum + 1.0) / (2.0 * called + 2.0)
    scale = 1.0 / jnp.sqrt(2.0 * freq * (1.0 - freq))
    standard = jnp.where(observed, (dosage - 2.0 * freq) * scale, 0.0).astype(jnp.bfloat16)
    row_count = genotype.shape[0]
    total = row_count * lax.axis_size("samp")
    contract = (((0,), (0,)), ((), ()))
    block = basis
    for step in range(ITERS):
        scores = lax.psum(jnp.dot(standard, block, preferred_element_type=jnp.float32), "snp")
        sample_scores = scores.astype(jnp.bfloat16)
        local = lax.dot_general(
            standard, sample_scores, contract, preferred_element_type=jnp.float32
        )
        snp_block = lax.psum(local, "samp") / total
        block = snp_block.astype(jnp.bfloat16)
    return (sample_scores, snp_block)


def solution(mesh):
    placed = (P("samp", "snp"), P("snp", None))
    return jax.shard_map(
        per_device,
        mesh=mesh,
        in_specs=placed,
        out_specs=(P("samp", None), P("snp", None)),
        check_vma=False,
    )
```

profile of v0, /device:TPU:8, one launch (start us, length us, event | category | flops | bytes accessed | tf_op | source)
XLA Modules:
  0.0 305.8 jit_solution(3003615969748180968)
XLA Ops:
  7.2 0.0 copy-start
  7.2 0.0 all-reduce.6.cloned.1.call-start
  7.2 5.1 %convert_reduce_fusion.1 = (f32[2048]{0:T(1024)S(1)}, f32[2048]{0:T(1024)S(1)}) fusion(s32[1024,2048]{1,0:T(8,128)} %param.2), kind=kLoop, calls=%fused_computation.2 | loop fusion | flops 12578816 | bytes 8404992 | tf_op jit(solution)/shard_map/reduce_sum | solution.py:13
  12.3 53.5 %all-reduce = (f32[2048]{0:T(1024)S(1)}, f32[2048]{0:T(1024)S(1)}) all-reduce(f32[2048]{0:T(1024)S(1)} %get-tuple-element.3, f32[2048]{0:T(1024)S(1)} %get-tuple-element.2), channel_id=1, replica_groups=mesh['samp'=16,'snp'=2] {'samp'}, use_global_device_ids=true, to_apply=%region_3.4 | all-reduce | flops 4096 | bytes 32768 | tf_op jit(solution)/shard_map/psum | solution.py:12
  65.8 4.4 %select_convert_fusion = bf16[1024,2048]{1,0:T(8,128)(2,1)S(1)} fusion(s32[1024,2048]{1,0:T(8,128)} %param.2, f32[2048]{0:T(1024)S(1)} %get-tuple-element.7, f32[2048]{0:T(1024)S(1)} %get-tuple-element.6), kind=kLoop, calls=%fused_computation | loop fusion | flops 14680064 | bytes 12599296 | tf_op jit(solution)/shard_map/convert_element_type | solution.py:17
  70.2 0.0 copy-start.1
  70.2 1.9 copy-done.1
  72.1 0.0 copy-done
  72.1 1.2 fusion.5
  73.4 15.7 %all-reduce.9 = bf16[1024,40]{1,0:T(8,128)(2,1)S(1)} all-reduce(f32[1024,40]{1,0:T(8,128)S(1)} %fusion.5), channel_id=1, replica_groups=mesh['samp'=16,'snp'=2] {'snp'}, use_global_device_ids=true, to_apply=%region_4.5 | all-reduce | flops 40960 | bytes 245760 | tf_op jit(solution)/shard_map/psum | solution.py:23
  89.0 3.8 %fusion.7 = f32[2048,40]{0,1:T(8,128)} fusion(bf16[1024,2048]{1,0:T(8,128)(2,1)} %copy-done.1, bf16[1024,40]{1,0:T(8,128)(2,1)S(1)} %all-reduce.9), kind=kOutput, calls=%fused_computation.16 | convolution fusion | flops 167772160 | bytes 4603904 | tf_op jit(solution)/shard_map/dot_general | solution.py:25
  92.8 0.0 all-reduce.6.cloned.1.call-update
  92.8 0.0 all-reduce.8.cloned.1.call-start
  92.9 96.7 %all-reduce.6.cloned.1.call-done = f32[2048,40]{0,1:T(8,128)} async-done(((f32[2048,40]{0,1:T(8,128)}), f32[2048,40]{0,1:T(8,128)}) %all-reduce.6.cloned.1.call-update) | async-done | bytes 327696 | tf_op jit(solution)/shard_map/psum | solution.py:28
  189.6 3.6 %fusion.2 = f32[1024,40]{0,1:T(8,128)S(1)} fusion(bf16[1024,2048]{1,0:T(8,128)(2,1)} %copy-done.1, f32[2048,40]{0,1:T(8,128)} %all-reduce.6.cloned.1.call-done), kind=kOutput, calls=%fused_computation.7 | convolution fusion | flops 167936000 | bytes 4685824 | tf_op jit(solution)/shard_map/dot_general | solution.py:23
  193.2 10.0 %all-reduce.10 = bf16[1024,40]{0,1:T(8,128)(2,1)S(1)} all-reduce(f32[1024,40]{0,1:T(8,128)S(1)} %fusion.2), channel_id=1, replica_groups=mesh['samp'=16,'snp'=2] {'snp'}, use_global_device_ids=true, to_apply=%region_6.7 | all-reduce | flops 40960 | bytes 245760 | tf_op jit(solution)/shard_map/psum | solution.py:23
  203.2 0.0 copy-start.2
  203.2 3.8 %fusion.6 = f32[2048,40]{0,1:T(8,128)} fusion(bf16[1024,2048]{1,0:T(8,128)(2,1)} %copy-done.1, bf16[1024,40]{0,1:T(8,128)(2,1)S(1)} %all-reduce.10), kind=kOutput, calls=%fused_computation.15 | convolution fusion | flops 167772160 | bytes 4603904 | tf_op jit(solution)/shard_map/dot_general | solution.py:25
  206.9 0.0 all-reduce.8.cloned.1.call-update
  207.0 90.2 %all-reduce.8.cloned.1.call-done = f32[2048,40]{0,1:T(8,128)} async-done(((f32[2048,40]{0,1:T(8,128)}), f32[2048,40]{0,1:T(8,128)}) %all-reduce.8.cloned.1.call-update) | async-done | bytes 327696 | tf_op jit(solution)/shard_map/psum | solution.py:28
  297.2 1.7 broadcast_multiply_fusion
  298.9 0.0 copy-done.2
  (1 shorter events, 0.0 us)
Async XLA Ops:
  7.2 65.0 %copy-start = (bf16[2048,40]{0,1:T(8,128)(2,1)S(1)}, bf16[2048,40]{0,1:T(8,128)(2,1)}, u32[]{:S(2)}) copy-start(bf16[2048,40]{0,1:T(8,128)(2,1)} %param.3) | copy-start | bytes 491524
  7.2 182.4 %all-reduce.6.cloned.1.call-start = ((), (), s32[]{:S(2)}) async-start(), calls=%async_computation | async-start | bytes 655360 | tf_op jit(solution)/shard_map/psum | solution.py:28
  70.2 1.9 copy-start.1
  92.8 204.4 %all-reduce.8.cloned.1.call-start = ((), (), s32[]{:S(2)}) async-start(), calls=%async_computation.1 | async-start | bytes 655360 | tf_op jit(solution)/shard_map/psum | solution.py:28
  203.2 95.8 %copy-start.2 = (bf16[1024,40]{0,1:T(8,128)(2,1)}, bf16[1024,40]{0,1:T(8,128)(2,1)S(1)}, u32[]{:S(2)}) copy-start(bf16[1024,40]{0,1:T(8,128)(2,1)S(1)} %all-reduce.10) | copy-start | bytes 245764
Sparse Core Ops, SparseCore 0:
  92.9 96.6 all-reduce.5
  207.1 90.0 all-reduce.7
where the time goes:
time: 306 us
  waiting for transfers between devices  187 us (61%)
  blocking collectives  79.1 us (26%)
  between operations  14.1 us (5%)
  matrix products  12.3 us (4%)
  other arithmetic  11.2 us (4%)
    psum x2, waiting for transfers between devices, per_device(): snp_block = lax.psum(local, 'samp') / total  187 us
    psum x1, blocking collectives, per_device(): lax.psum((jnp.sum(dosage, axis=0), jnp.sum(observed.astype(jnp.float32),...  53.5 us
    psum x2, blocking collectives, per_device(): lax.psum(jnp.dot(standard, block, preferred_element_type=jnp.float32), 's...  25.6 us
    dot_general x2, matrix products, per_device(): lax.dot_general(standard, sample_scores, contract, preferred_element_type...  7.52 us
  transfers between devices with their start and end apart: 2, of which 2 were waited for; matrix products, arithmetic and copies ran while one was open for 0% of the time, Pallas kernels for 0%

commit v1 on v0

--- a/solution.py
+++ b/solution.py
@@ -4,6 +4,12 @@
 from jax.sharding import PartitionSpec as P
 
 ITERS = 2
+
+
+def meshes_move(dev_axis, load):
+    work_now = jax.lax.all_gather(load, dev_axis)
+    seen_now = jnp.sum(work_now, axis=0)
+    return seen_now
 
 
 def per_device(genotype, basis):
@@ -25,7 +31,7 @@
         local = lax.dot_general(
             standard, sample_scores, contract, preferred_element_type=jnp.float32
         )
-        snp_block = lax.psum(local, "samp") / total
+        snp_block = meshes_move("samp", local) / total
         block = snp_block.astype(jnp.bfloat16)
     return (sample_scores, snp_block)
 

time: 306 us -> 247 us (0.81)
  waiting for transfers between devices: 187 us -> 115 us
  local copies, waits for them, and re-layouts: 1.93 us -> 14.2 us
    psum x2 -> x0, waiting for transfers between devices: 187 us -> none  [per_device(): snp_block = lax.psum(local, 'samp') / total]
    all_gather x0 -> x2, waiting for transfers between devices: none -> 115 us  [meshes_move(): work_now = jax.lax.all_gather(load, dev_axis)]
    unnamed x6 -> x10, local copies, waits for them, and re-layouts: 1.93 us -> 14.2 us
where the time goes in v1:
time: 247 us; the launch traced here: 245 us
  waiting for transfers between devices  115 us (47%)
  blocking collectives  79.5 us (32%)
  local copies, waits for them, and re-layouts  14.2 us (6%)
  between operations  14.1 us (6%)
  other arithmetic  12.1 us (5%)
  matrix products  10.1 us (4%)
    all_gather x2, waiting for transfers between devices, meshes_move(): work_now = jax.lax.all_gather(load, dev_axis)  115 us
    psum x1, blocking collectives, per_device(): lax.psum((jnp.sum(dosage, axis=0), jnp.sum(observed.astype(jnp.float32),...  53.5 us
    psum x2, blocking collectives, per_device(): lax.psum(jnp.dot(standard, block, preferred_element_type=jnp.float32), 's...  26 us
    unnamed x10, local copies, waits for them, and re-layouts  14.2 us
    dot_general x2, matrix products, per_device(): lax.dot_general(standard, sample_scores, contract, preferred_element_type...  7.52 us
    reduce_sum x1, other arithmetic, per_device(): jnp.sum(dosage, axis=0)  5.06 us
  transfers between devices with their start and end apart: 2, of which 2 were waited for; matrix products, arithmetic and copies ran while one was open for 0% of the time, Pallas kernels for 0%

profile of v1, /device:TPU:8, one launch (start us, length us, event | category | flops | bytes accessed | tf_op | source)
XLA Modules:
  0.0 244.8 jit_solution(1473212002994971361)
XLA Ops:
  7.2 0.0 copy-start
  7.2 0.0 all-gather.5.cloned.1.call-start
  7.2 5.1 %convert_reduce_fusion.1 = (f32[2048]{0:T(1024)S(1)}, f32[2048]{0:T(1024)S(1)}) fusion(s32[1024,2048]{1,0:T(8,128)} %param.2), kind=kLoop, calls=%fused_computation.2 | loop fusion | flops 12578816 | bytes 8404992 | tf_op jit(solution)/shard_map/reduce_sum | solution.py:19
  12.3 53.5 %all-reduce = (f32[2048]{0:T(1024)S(1)}, f32[2048]{0:T(1024)S(1)}) all-reduce(f32[2048]{0:T(1024)S(1)} %get-tuple-element.3, f32[2048]{0:T(1024)S(1)} %get-tuple-element.2), channel_id=1, replica_groups=mesh['samp'=16,'snp'=2] {'samp'}, use_global_device_ids=true, to_apply=%region_3.4 | all-reduce | flops 4096 | bytes 32768 | tf_op jit(solution)/shard_map/psum | solution.py:18
  65.8 4.4 %select_convert_fusion = bf16[1024,2048]{1,0:T(8,128)(2,1)S(1)} fusion(s32[1024,2048]{1,0:T(8,128)} %param.2, f32[2048]{0:T(1024)S(1)} %get-tuple-element.7, f32[2048]{0:T(1024)S(1)} %get-tuple-element.6), kind=kLoop, calls=%fused_computation | loop fusion | flops 14680064 | bytes 12599296 | tf_op jit(solution)/shard_map/convert_element_type | solution.py:23
  70.2 2.0 copy-done.1
  72.2 1.2 fusion.5
  73.5 15.7 %all-reduce.3 = bf16[1024,40]{1,0:T(8,128)(2,1)S(1)} all-reduce(f32[1024,40]{1,0:T(8,128)S(1)} %fusion.5), channel_id=1, replica_groups=mesh['samp'=16,'snp'=2] {'snp'}, use_global_device_ids=true, to_apply=%region_4.5 | all-reduce | flops 40960 | bytes 245760 | tf_op jit(solution)/shard_map/psum | solution.py:29
  89.1 3.8 %fusion.7 = f32[2048,40]{0,1:T(8,128)} fusion(bf16[1024,2048]{1,0:T(8,128)(2,1)} %copy-done.1, bf16[1024,40]{1,0:T(8,128)(2,1)S(1)} %all-reduce.3), kind=kOutput, calls=%fused_computation.18 | convolution fusion | flops 167772160 | bytes 4603904 | tf_op jit(solution)/shard_map/dot_general | solution.py:31
  92.9 0.0 all-gather.5.cloned.1.call-update
  92.9 0.0 all-gather.7.cloned.1.call-start
  93.0 61.1 %all-gather.5.cloned.1.call-done = f32[32768,40]{0,1:T(8,128)} async-done(((f32[2048,40]{0,1:T(8,128)}), f32[32768,40]{0,1:T(8,128)}) %all-gather.5.cloned.1.call-update) | async-done | bytes 5242896 | tf_op jit(solution)/shard_map/all_gather | solution.py:10
  154.1 5.5 %copy.4 = f32[5,8,16,2048]{3,2,1,0:T(8,128)S(1)} copy(f32[5,8,16,2048]{3,1,2,0:T(8,128)} %bitcast.17) | data formatting | bytes 10485760
  159.5 0.9 bitcast_reduce_fusion.1
  160.5 1.2 copy-done.2
  161.7 1.4 fusion.2
  163.1 10.3 %all-reduce.4 = bf16[1024,40]{0,1:T(8,128)(2,1)S(1)} all-reduce(f32[1024,40]{0,1:T(8,128)S(1)} %fusion.2), channel_id=1, replica_groups=mesh['samp'=16,'snp'=2] {'snp'}, use_global_device_ids=true, to_apply=%region_6.7 | all-reduce | flops 40960 | bytes 245760 | tf_op jit(solution)/shard_map/psum | solution.py:29
  173.4 0.0 copy-start.3
  173.4 3.8 %fusion.6 = f32[2048,40]{0,1:T(8,128)} fusion(bf16[1024,2048]{1,0:T(8,128)(2,1)} %copy-done.1, bf16[1024,40]{0,1:T(8,128)(2,1)S(1)} %all-reduce.4), kind=kOutput, calls=%fused_computation.17 | convolution fusion | flops 167772160 | bytes 4603904 | tf_op jit(solution)/shard_map/dot_general | solution.py:31
  177.2 0.0 all-gather.7.cloned.1.call-update
  177.2 53.6 %all-gather.7.cloned.1.call-done = f32[32768,40]{0,1:T(8,128)} async-done(((f32[2048,40]{0,1:T(8,128)}), f32[32768,40]{0,1:T(8,128)}) %all-gather.7.cloned.1.call-update) | async-done | bytes 5242896 | tf_op jit(solution)/shard_map/all_gather | solution.py:10
  230.8 5.5 %copy.5 = f32[5,8,16,2048]{3,2,1,0:T(8,128)S(1)} copy(f32[5,8,16,2048]{3,1,2,0:T(8,128)} %bitcast.18) | data formatting | bytes 10485760
  236.3 0.9 bitcast_reduce_fusion
  237.2 0.7 broadcast_multiply_fusion
  (5 shorter events, 0.0 us)
Async XLA Ops:
  7.2 65.1 %copy-start = (bf16[2048,40]{0,1:T(8,128)(2,1)S(1)}, bf16[2048,40]{0,1:T(8,128)(2,1)}, u32[]{:S(2)}) copy-start(bf16[2048,40]{0,1:T(8,128)(2,1)} %param.3) | copy-start | bytes 491524
  7.2 146.9 %all-gather.5.cloned.1.call-start = ((), (), s32[]{:S(2)}) async-start(), calls=%async_computation | async-start | bytes 5570560 | tf_op jit(solution)/shard_map/all_gather | solution.py:10
  70.2 2.0 copy-start.1
  92.9 137.9 %all-gather.7.cloned.1.call-start = ((), (), s32[]{:S(2)}) async-start(), calls=%async_computation.1 | async-start | bytes 5570560 | tf_op jit(solution)/shard_map/all_gather | solution.py:10
  159.5 2.2 copy-start.2
  173.4 62.9 %copy-start.3 = (bf16[1024,40]{0,1:T(8,128)(2,1)}, bf16[1024,40]{0,1:T(8,128)(2,1)S(1)}, u32[]{:S(2)}) copy-start(bf16[1024,40]{0,1:T(8,128)(2,1)S(1)} %all-reduce.4) | copy-start | bytes 245764
Sparse Core Ops, SparseCore 0:
  93.0 60.9 all-gather.4
  177.3 53.4 all-gather.6
